TPU v7x, 32 devices: a whole 2x2x4 slice. The times are simulated.
32 devices in a mesh: pair: 8 (over z, core), orb: 4 (over y, x).
Axes of the slice: x: 2, y: 2, z: 4, core: 2. Of those that a mesh axis runs over, the one named last changes fastest.
Arguments:
- amplitudes: float32 [128, 128, 128], P(('pair', 'orb')), may hold values from -3 to 3
- couple: int32 [128, 16], P(('pair', 'orb')), may hold values from 0 to 127, as said below
- occ_first: int32 [128], P('pair'), may hold values from 0 to 31, as said below
- occ_second: int32 [128], P('pair'), may hold values from 0 to 31, as said below
- couple_intersection: bfloat16 [128, 16, 128, 128], P(('pair', 'orb')), may hold values from -0.375 to 0.375
- pno_maps: bfloat16 [128, 2, 128, 128], P('pair'), may hold values from -0.5 to 0.5
- orbital_blocks: bfloat16 [32, 512, 128], P('pair', 'orb'), may hold values from -2 to 2
- pno_energy: float32 [128, 128], P(('pair', 'orb')), may hold values from 0.5 to 2.5
- occ_energy: float32 [32], replicated, may hold values from -1.5 to -0.3
Outputs:
- new_amplitudes: float32 [128, 128, 128], P(('pair', 'orb'))
- dressed: float32 [32, 512, 128], P('pair', 'orb')
Inputs may be any that keep to these rules, and one draw needn't show every extreme that they name: `couple`: every listed partner of a pair lies in the same pair group as the pair (pairs g * 16 to (g + 1) * 16 - 1 form group g). `occ_first`: the pairs of group g have first orbitals in g * 4 to (g + 1) * 4 - 1. `occ_second`: the pairs of group g have second orbitals among the orbitals of groups g - 1 to g + 1, counted modulo 8 (group h holds orbitals h * 4 to (h + 1) * 4 - 1).
All inputs are finite; a program needn't handle non-finite values.
Results may differ from a plain program's by a relative error of at most 0.014.
Values may be sent and summed in bfloat16 or wider, within the bound.
A program may use at most 64 MiB of HBM per device.

v0:
```python
import jax
import jax.numpy as jnp
from jax import lax
from jax.sharding import PartitionSpec as P

REACH = 1
ITERS = 2


dress_scale = 0.015


def extended(block, sides, width):
    for axis, dim in sides:
        count = lax.axis_size(axis)
        forward = [(i, i + 1) for i in range(count - 1)]
        forward.append((count - 1, 0))
        backward = [(target, source) for source, target in forward]
        low = lax.ppermute(
            lax.slice_in_dim(block, block.shape[dim] - width, None, axis=dim), axis, forward
        )
        high = lax.ppermute(lax.slice_in_dim(block, 0, width, axis=dim), axis, backward)
        block = jnp.concatenate([low, block, high], axis=dim)
    return block


def pick_window(window, second_ids, orb_count):
    owners = lax.axis_size("pair")
    group_here = lax.axis_index("pair")
    owner_ids = second_ids // orb_count
    distance = (owner_ids - group_here + REACH + owners) % owners
    position = distance * orb_count + second_ids % orb_count
    return jnp.take(window, position, axis=0)


def on_device(
    amplitudes,
    couple,
    occ_first,
    occ_second,
    couple_intersection,
    pno_maps,
    orbital_blocks,
    pno_energy,
    occ_energy,
):
    pair_count = amplitudes.shape[0]
    group_size = occ_first.shape[0]
    orb_count = orbital_blocks.shape[0]
    offset = lax.axis_index("orb") * pair_count
    first_local = occ_first % orb_count
    own_first = lax.dynamic_slice_in_dim(occ_first, offset, pair_count)
    own_second = lax.dynamic_slice_in_dim(occ_second, offset, pair_count)
    labels = jnp.arange(occ_energy.shape[0], dtype=jnp.int32)
    first_energy = jnp.sum(
        jnp.where(own_first[:, None] == labels[None, :], occ_energy[None, :], 0.0), axis=1
    )
    second_energy = jnp.sum(
        jnp.where(own_second[:, None] == labels[None, :], occ_energy[None, :], 0.0), axis=1
    )
    denominator = pno_energy[:, :, None] + pno_energy[:, None, :]
    denominator = denominator - first_energy[:, None, None] - second_energy[:, None, None]
    partner_ids = couple % group_size
    onehot = (first_local[None, :] == jnp.arange(orb_count, dtype=jnp.int32)[:, None]).astype(
        jnp.float32
    )
    bare_blocks = orbital_blocks.astype(jnp.float32)
    dressed = bare_blocks
    amps_now = amplitudes
    for iteration in range(ITERS):
        amp_half = lax.all_gather(amps_now.astype(jnp.bfloat16), "orb", axis=0, tiled=True)
        block_half = dressed.astype(jnp.bfloat16)
        first_blocks = jnp.take(block_half, first_local, axis=0)
        window = extended(block_half, (("pair", 0),), REACH * orb_count)
        second_blocks = pick_window(window, occ_second, orb_count)
        first_projected = jnp.einsum(
            "pqa,pab->pqb", first_blocks, pno_maps[:, 0], preferred_element_type=jnp.float32
        ).astype(jnp.bfloat16)
        second_projected = jnp.einsum(
            "pqa,pab->pqb", second_blocks, pno_maps[:, 1], preferred_element_type=jnp.float32
        ).astype(jnp.bfloat16)
        integrals = lax.psum_scatter(
            jnp.einsum(
                "pqa,pqb->pab",
                first_projected,
                second_projected,
                preferred_element_type=jnp.float32,
            ).astype(jnp.bfloat16),
            "orb",
            scatter_dimension=0,
            tiled=True,
        ).astype(jnp.float32)
        partners = jnp.take(amp_half, partner_ids.reshape(-1), axis=0)
        partners = partners.reshape(partner_ids.shape + amp_half.shape[1:])
        half_products = jnp.einsum(
            "pkab,pkbc->pkac", couple_intersection, partners, preferred_element_type=jnp.float32
        ).astype(jnp.bfloat16)
        coupled = jnp.einsum(
            "pkac,pkdc->pad", half_products, couple_intersection, preferred_element_type=jnp.float32
        )
        fitted_half = jnp.einsum(
            "pqa,pab->pqb", second_projected, amp_half, preferred_element_type=jnp.float32
        ).astype(jnp.bfloat16)
        returned = jnp.einsum(
            "pqb,pcb->pqc", fitted_half, pno_maps[:, 0], preferred_element_type=jnp.float32
        )
        fitted = jnp.einsum("op,pqc->oqc", onehot, returned, precision=lax.Precision.HIGHEST)
        dressed = bare_blocks + dress_scale * fitted
        amps_now = -(integrals + coupled) / denominator
    return (amps_now, dressed)


def solution(mesh):
    return jax.shard_map(
        on_device,
        mesh=mesh,
        in_specs=(
            P(("pair", "orb"), None, None),
            P(("pair", "orb"), None),
            P("pair"),
            P("pair"),
            P(("pair", "orb"), None, None, None),
            P("pair", None, None, None),
            P("pair", "orb", None),
            P(("pair", "orb"), None),
            P(),
        ),
        out_specs=(P(("pair", "orb"), None, None), P("pair", "orb", None)),
        check_vma=False,
    )
```

profile of v0, /device:TPU:0, one launch (start us, length us, event | category | flops | bytes accessed | tf_op | source)
XLA Modules:
  0.0 107.2 jit_solution(8851082411708992334)
XLA Ops:
  7.2 0.0 copy-start
  7.2 0.0 reduce-scatter.5.cloned.1.call-start
  7.2 4.6 %collective-permute-start.1 = (bf16[4,128,128]{2,1,0:T(8,128)(2,1)}, bf16[4,128,128]{2,1,0:T(8,128)(2,1)S(1)}, u32[]{:S(2)}, u32[]{:S(2)}) collective-permute-start(bf16[4,128,128]{2,1,0:T(8,128)(2,1)} %param.21), channel_id=1, source_target_pairs={{4,0},{8,4},{12,8},{16,12},{20,16},{24,20},{28,24},{0,28},{5,1},{9... | collective-permute-start | bytes 393224 | tf_op jit(solution)/shard_map/ppermute | solution.py:22
  11.8 0.0 collective-permute-start
  11.8 0.7 add_select_fusion
  12.5 0.1 reshape.37
  12.6 0.7 compare_and_fusion.1
  13.3 1.0 convert_element_type.58
  14.3 0.7 compare_and_fusion.2
  15.0 10.1 %all_gather.6 = bf16[16,128,128]{2,1,0:T(8,128)(2,1)S(1)} all-gather(bf16[4,128,128]{2,1,0:T(8,128)(2,1)S(1)} %convert_element_type.58), channel_id=1, replica_groups=mesh['pair'=8,'orb'=4] {'orb'}, dimensions={0}, use_global_device_ids=true | all-gather | bytes 655360 | tf_op jit(solution)/shard_map/all_gather | solution.py:71
  25.1 2.3 %gather_fusion.3 = bf16[16,128,128]{2,1,0:T(8,128)(2,1)} fusion(bf16[4,128,128]{2,1,0:T(8,128)(2,1)} %param.21, s32[1024]{0:T(1024)S(1)} %pad_clamp_fusion.1), kind=kCustom, calls=%fused_computation.4.clone | custom fusion | bytes 1048640 | tf_op jit(solution)/shard_map/jit(_take)/gather | solution.py:73
  27.4 2.2 %gather_fusion.4 = bf16[64,128,128]{2,1,0:T(8,128)(2,1)} fusion(bf16[16,128,128]{2,1,0:T(8,128)(2,1)S(1)} %all_gather.6, s32[1024]{0:T(1024)S(1)} %pad_clamp_fusion), kind=kCustom, calls=%fused_computation.2.clone | custom fusion | bytes 4194560 | tf_op jit(solution)/shard_map/jit(_take)/gather | solution.py:93
  29.6 0.0 collective-permute-done.1
  29.6 0.0 collective-permute-done
  29.6 1.4 %gather_fusion = bf16[16,128,128]{2,1,0:T(8,128)(2,1)} fusion(bf16[12,128,128]{2,1,0:T(8,128)(2,1)S(1)} %pad_maximum_fusion.1, s32[1024]{0:T(1024)S(1)} %pad_clamp_fusion.2), kind=kCustom, calls=%fused_computation.clone | custom fusion | bytes 1048640 | tf_op jit(solution)/shard_map/jit(_take)/gather | solution.py:33
  31.1 1.6 %convolution_convert_fusion.7 = bf16[16,128,128]{2,1,0:T(8,128)(2,1)S(1)} fusion(bf16[16,128,128]{2,1,0:T(8,128)(2,1)} %gather_fusion, pred[16]{0:T(512)(128)(4,1)S(1)} %get-tuple-element.17, bf16[16,2,128,128]{3,2,1,0:T(8,128)(2,1)} %param.20), kind=kOutput, calls=%fused_computation.23 | convolution fusion | flops 67633152 | bytes 1572880 | tf_op jit(solution)/shard_map/pqa,pab->pqb/dot_general | solution.py:79
  32.6 2.7 %fusion.10 = f32[16,128,128]{2,1,0:T(8,128)} fusion(bf16[16,128,128]{2,1,0:T(8,128)(2,1)S(1)} %convolution_convert_fusion.7, bf16[16,128,128]{2,1,0:T(8,128)(2,1)S(1)} %all_gather.6, bf16[16,2,128,128]{3,2,1,0:T(8,128)(2,1)} %param.20), kind=kOutput, calls=%fused_computation.24 | convolution fusion | flops 134479872 | bytes 2621440 | tf_op jit(solution)/shard_map/pqb,pcb->pqc/dot_general | solution.py:104
  35.3 2.3 %fusion.41 = bf16[4,128,128]{2,0,1:T(4,128)(2,1)S(1)} fusion(f32[16,128,128]{2,1,0:T(8,128)} %fusion.10, bf16[4,128,128]{2,1,0:T(8,128)(2,1)S(1)} %copy-done.1, s32[16]{0:T(128)S(1)} %get-tuple-element.16), kind=kOutput, calls=%fused_computation.39 | convolution fusion | flops 12845120 | bytes 1310784 | tf_op jit(solution)/shard_map/op,pqc->oqc/dot_general | solution.py:107
  37.6 1.9 %collective-permute-start.3 = (bf16[4,128,128]{2,0,1:T(4,128)(2,1)S(1)}, bf16[4,128,128]{2,0,1:T(4,128)(2,1)S(1)}, u32[]{:S(2)}, u32[]{:S(2)}) collective-permute-start(bf16[4,128,128]{2,0,1:T(4,128)(2,1)S(1)} %fusion.41), channel_id=1, source_target_pairs={{4,0},{8,4},{12,8},{16,12},{20,16},{24,20},{28,24},{0,28},{5,1},{9... | collective-permute-start | bytes 393224 | tf_op jit(solution)/shard_map/ppermute | solution.py:22
  39.5 2.6 %convolution_convert_fusion.1 = bf16[16,128,128]{2,1,0:T(8,128)(2,1)} fusion(bf16[16,128,128]{2,1,0:T(8,128)(2,1)S(1)} %convolution_convert_fusion.7, bf16[16,128,128]{2,1,0:T(8,128)(2,1)} %gather_fusion.3, pred[16]{0:T(512)(128)(4,1)S(1)} %get-tuple-element.15, bf16[16,2,128,128]{3,2,1,0:T(8,128)(2,1)} %param.20), kind=kOutput, calls=%fused_computation.17 | convolution fusion | flops 135004160 | bytes 2097168 | tf_op jit(solution)/shard_map/pqa,pqb->pab/dot_general | solution.py:83
  42.1 0.0 reduce-scatter.5.cloned.1.call-update
  42.1 0.0 copy-start.5
  42.1 0.0 copy-start.3
  42.1 0.0 copy-start.2
  42.1 0.0 reduce-scatter.3.cloned.1.call-start
  42.2 3.2 %broadcast_select_fusion = bf16[64,128,128]{2,1,0:T(8,128)(2,1)} fusion(bf16[64,128,128]{2,1,0:T(8,128)(2,1)} %gather_fusion.4, pred[64]{0:T(512)(128)(4,1)S(1)} %compare_and_fusion), kind=kLoop, calls=%fused_computation.14 | loop fusion | flops 1048576 | bytes 4194368 | tf_op jit(solution)/shard_map/jit(_take)/select_n | solution.py:93
  45.4 0.1 dynamic_slice.6
  45.4 0.1 dynamic_slice.7
  45.5 0.2 select_reduce_fusion.1
  45.8 1.4 %gather_fusion.1 = bf16[16,128,128]{2,1,0:T(8,128)(2,1)} fusion(bf16[4,128,128]{2,1,0:T(8,128)(2,1)S(1)} %copy.38, s32[1024]{0:T(1024)S(1)} %pad_clamp_fusion.1), kind=kCustom, calls=%fused_computation.1.clone | custom fusion | bytes 1048640 | tf_op jit(solution)/shard_map/jit(_take)/gather | solution.py:73
  47.2 0.0 collective-permute-done.3
  47.2 0.0 collective-permute-done.2
  47.2 0.3 pad_maximum_fusion
  47.5 0.1 copy.39
  47.6 1.4 %gather_fusion.2 = bf16[16,128,128]{2,1,0:T(8,128)(2,1)} fusion(bf16[12,128,128]{2,1,0:T(8,128)(2,1)S(1)} %copy.39, s32[1024]{0:T(1024)S(1)} %pad_clamp_fusion.2), kind=kCustom, calls=%fused_computation.3.clone | custom fusion | bytes 1048640 | tf_op jit(solution)/shard_map/jit(_take)/gather | solution.py:33
  49.0 1.6 %convolution_convert_fusion.4 = bf16[16,128,128]{2,1,0:T(8,128)(2,1)S(1)} fusion(bf16[16,128,128]{2,1,0:T(8,128)(2,1)} %gather_fusion.2, pred[16]{0:T(512)(128)(4,1)S(1)} %get-tuple-element.17, bf16[16,2,128,128]{3,2,1,0:T(8,128)(2,1)} %param.20), kind=kOutput, calls=%fused_computation.20 | convolution fusion | flops 67633152 | bytes 1572880 | tf_op jit(solution)/shard_map/pqa,pab->pqb/dot_general | solution.py:79
  50.5 2.6 %convolution_convert_fusion.3 = bf16[16,128,128]{2,1,0:T(8,128)(2,1)} fusion(bf16[16,128,128]{2,1,0:T(8,128)(2,1)S(1)} %convolution_convert_fusion.4, bf16[16,128,128]{2,1,0:T(8,128)(2,1)} %gather_fusion.1, pred[16]{0:T(512)(128)(4,1)S(1)} %get-tuple-element.15, bf16[16,2,128,128]{3,2,1,0:T(8,128)(2,1)} %param.20), kind=kOutput, calls=%fused_computation.19 | convolution fusion | flops 135004160 | bytes 2097168 | tf_op jit(solution)/shard_map/pqa,pqb->pab/dot_general | solution.py:83
  53.1 0.0 reduce-scatter.3.cloned.1.call-update
  53.1 14.5 %reduce-scatter.5.cloned.1.call-done = bf16[4,128,128]{2,1,0:T(8,128)(2,1)} async-done(((bf16[16,128,128]{2,1,0:T(8,128)(2,1)}), bf16[4,128,128]{2,1,0:T(8,128)(2,1)}) %reduce-scatter.5.cloned.1.call-update) | async-done | bytes 131088 | tf_op jit(solution)/shard_map/reduce_scatter | solution.py:82
  67.6 3.7 %fusion.38 = bf16[4,128,128]{2,1,0:T(8,128)(2,1)S(1)} fusion(bf16[4,16,128,128]{3,2,1,0:T(8,128)(2,1)S(1)} %copy-done, bf16[4,16,128,128]{3,2,1,0:T(8,128)(2,1)} %bitcast.82, bf16[4,128,128]{2,1,0:T(8,128)(2,1)} %reduce-scatter.5.cloned.1.call-done, f32[4]{0:T(128)S(1)} %get-tuple-element.14, f32[4]{0:T(128)S(1)} %get-tuple-element.13, ...), kind=kOutput, calls=%fused_computation.38 | convolution fusion | flops 538443776 | bytes 4458528 | tf_op jit(solution)/shard_map/pkac,pkdc->pad/dot_general | solution.py:98
  71.3 10.5 %all_gather.7 = bf16[16,128,128]{2,1,0:T(8,128)(2,1)S(1)} all-gather(bf16[4,128,128]{2,1,0:T(8,128)(2,1)S(1)} %fusion.38), channel_id=1, replica_groups=mesh['pair'=8,'orb'=4] {'orb'}, dimensions={0}, use_global_device_ids=true | all-gather | bytes 655360 | tf_op jit(solution)/shard_map/all_gather | solution.py:71
  81.8 2.2 %gather_fusion.5 = bf16[64,128,128]{2,1,0:T(8,128)(2,1)} fusion(bf16[16,128,128]{2,1,0:T(8,128)(2,1)S(1)} %all_gather.7, s32[1024]{0:T(1024)S(1)} %pad_clamp_fusion), kind=kCustom, calls=%fused_computation.5.clone | custom fusion | bytes 4194560 | tf_op jit(solution)/shard_map/jit(_take)/gather | solution.py:93
  84.0 2.7 %fusion.11 = f32[16,128,128]{2,1,0:T(8,128)} fusion(bf16[16,128,128]{2,1,0:T(8,128)(2,1)S(1)} %convolution_convert_fusion.4, bf16[16,128,128]{2,1,0:T(8,128)(2,1)S(1)} %all_gather.7, bf16[16,2,128,128]{3,2,1,0:T(8,128)(2,1)} %param.20), kind=kOutput, calls=%fused_computation.25 | convolution fusion | flops 134479872 | bytes 2621440 | tf_op jit(solution)/shard_map/pqb,pcb->pqc/dot_general | solution.py:104
  86.7 2.3 %fusion.19 = f32[4,128,128]{2,0,1:T(4,128)S(1)} fusion(f32[16,128,128]{2,1,0:T(8,128)} %fusion.11, bf16[4,128,128]{2,1,0:T(8,128)(2,1)S(1)} %copy-done.1, s32[16]{0:T(128)S(1)} %get-tuple-element.16), kind=kOutput, calls=%fused_computation.31 | convolution fusion | flops 12779584 | bytes 1441856 | tf_op jit(solution)/shard_map/op,pqc->oqc/dot_general | solution.py:107
  89.0 0.7 copy.47
  89.7 3.2 %broadcast_select_fusion.1 = bf16[64,128,128]{2,1,0:T(8,128)(2,1)} fusion(bf16[64,128,128]{2,1,0:T(8,128)(2,1)} %gather_fusion.5, pred[64]{0:T(512)(128)(4,1)S(1)} %compare_and_fusion), kind=kLoop, calls=%fused_computation.15 | loop fusion | flops 1048576 | bytes 4194368 | tf_op jit(solution)/shard_map/jit(_take)/select_n | solution.py:93
  92.9 3.1 %reduce-scatter.3.cloned.1.call-done = bf16[4,128,128]{2,1,0:T(8,128)(2,1)} async-done(((bf16[16,128,128]{2,1,0:T(8,128)(2,1)}), bf16[4,128,128]{2,1,0:T(8,128)(2,1)}) %reduce-scatter.3.cloned.1.call-update) | async-done | bytes 131088 | tf_op jit(solution)/shard_map/reduce_scatter | solution.py:82
  96.0 4.4 %fusion.26 = f32[4,128,128]{2,1,0:T(8,128)} fusion(bf16[4,16,128,128]{3,2,1,0:T(8,128)(2,1)S(1)} %copy-done, bf16[4,16,128,128]{3,2,1,0:T(8,128)(2,1)} %bitcast.83, bf16[4,128,128]{2,1,0:T(8,128)(2,1)} %reduce-scatter.3.cloned.1.call-done, f32[4]{0:T(128)S(1)} %get-tuple-element.14, f32[4]{0:T(128)S(1)} %get-tuple-element.13, f32[4,128]{1,0:T(4,128)S(1)} %copy-done.4), kind=kOutput, calls=%fused_computation.34 | convolution fusion | flops 538378240 | bytes 4589600 | tf_op jit(solution)/shard_map/pkac,pkdc->pad/dot_general | solution.py:98
  (17 shorter events, 0.1 us)
Async XLA Ops:
  7.2 60.5 %copy-start = (bf16[4,16,128,128]{3,2,1,0:T(8,128)(2,1)S(1)}, bf16[4,16,128,128]{3,2,1,0:T(8,128)(2,1)}, u32[]{:S(2)}) copy-start(bf16[4,16,128,128]{3,2,1,0:T(8,128)(2,1)} %param.19) | copy-start | bytes 6291460
  7.2 60.4 %reduce-scatter.5.cloned.1.call-start = ((), (), s32[]{:S(2)}) async-start(), calls=%async_computation.3 | async-start | bytes 655360 | tf_op jit(solution)/shard_map/reduce_scatter | solution.py:82
  7.2 22.3 %collective-permute-start.1 = (bf16[4,128,128]{2,1,0:T(8,128)(2,1)}, bf16[4,128,128]{2,1,0:T(8,128)(2,1)S(1)}, u32[]{:S(2)}, u32[]{:S(2)}) collective-permute-start(bf16[4,128,128]{2,1,0:T(8,128)(2,1)} %param.21), channel_id=1, source_target_pairs={{4,0},{8,4},{12,8},{16,12},{20,16},{24,20},{28,24},{0,28},{5,1},{9... | collective-permute-start | bytes 393224 | tf_op jit(solution)/shard_map/ppermute | solution.py:22
  11.8 17.8 %collective-permute-start = (bf16[4,128,128]{2,1,0:T(8,128)(2,1)}, bf16[4,128,128]{2,1,0:T(8,128)(2,1)S(1)}, u32[]{:S(2)}, u32[]{:S(2)}) collective-permute-start(bf16[4,128,128]{2,1,0:T(8,128)(2,1)} %param.21), channel_id=1, source_target_pairs={{0,4},{4,8},{8,12},{12,16},{16,20},{20,24},{24,28},{28,0},{1,5},{5... | collective-permute-start | bytes 393224 | tf_op jit(solution)/shard_map/ppermute | solution.py:19
  27.4 2.2 %copy-start.1 = (bf16[4,128,128]{2,1,0:T(8,128)(2,1)S(1)}, bf16[4,128,128]{2,1,0:T(8,128)(2,1)}, u32[]{:S(2)}) copy-start(bf16[4,128,128]{2,1,0:T(8,128)(2,1)} %param.21) | copy-start | bytes 393220
  37.6 9.6 %collective-permute-start.3 = (bf16[4,128,128]{2,0,1:T(4,128)(2,1)S(1)}, bf16[4,128,128]{2,0,1:T(4,128)(2,1)S(1)}, u32[]{:S(2)}, u32[]{:S(2)}) collective-permute-start(bf16[4,128,128]{2,0,1:T(4,128)(2,1)S(1)} %fusion.41), channel_id=1, source_target_pairs={{4,0},{8,4},{12,8},{16,12},{20,16},{24,20},{28,24},{0,28},{5,1},{9... | collective-permute-start | bytes 393224 | tf_op jit(solution)/shard_map/ppermute | solution.py:22
  39.5 7.7 %collective-permute-start.2 = (bf16[4,128,128]{2,0,1:T(4,128)(2,1)S(1)}, bf16[4,128,128]{2,0,1:T(4,128)(2,1)S(1)}, u32[]{:S(2)}, u32[]{:S(2)}) collective-permute-start(bf16[4,128,128]{2,0,1:T(4,128)(2,1)S(1)} %fusion.41), channel_id=1, source_target_pairs={{0,4},{4,8},{8,12},{12,16},{16,20},{20,24},{24,28},{28,0},{1,5},{5... | collective-permute-start | bytes 393224 | tf_op jit(solution)/shard_map/ppermute | solution.py:19
  42.1 3.3 %copy-start.5 = (s32[16]{0:T(128)S(1)}, s32[16]{0:T(128)}, u32[]{:S(2)}) copy-start(s32[16]{0:T(128)} %param.17) | copy-start | bytes 196
  42.1 3.3 %copy-start.3 = (s32[16]{0:T(128)S(1)}, s32[16]{0:T(128)}, u32[]{:S(2)}) copy-start(s32[16]{0:T(128)} %param.18) | copy-start | bytes 196
  42.1 3.4 %copy-start.2 = (f32[32]{0:T(128)S(1)}, f32[32]{0:T(128)}, u32[]{:S(2)}) copy-start(f32[32]{0:T(128)} %param.23) | copy-start | bytes 388
  42.1 53.9 %reduce-scatter.3.cloned.1.call-start = ((), (), s32[]{:S(2)}) async-start(), calls=%async_computation.2 | async-start | bytes 655360 | tf_op jit(solution)/shard_map/reduce_scatter | solution.py:82
  49.0 18.7 %copy-start.4 = (f32[4,128]{1,0:T(4,128)S(1)}, f32[4,128]{1,0:T(4,128)}, u32[]{:S(2)}) copy-start(f32[4,128]{1,0:T(4,128)} %param.22) | copy-start | bytes 6148
Sparse Core Ops, SparseCore 0:
  42.2 25.3 reduce-scatter.4
  70.4 25.5 reduce-scatter.2
where the time goes:
time: 108 us; the launch traced here: 107 us
  matrix products  26.3 us (24%)
  blocking collectives  20.6 us (19%)
  waiting for transfers between devices  17.7 us (16%)
  between operations  14.2 us (13%)
  local copies, waits for them, and re-layouts  12 us (11%)
  other arithmetic  9.95 us (9%)
  starting transfers between devices  6.54 us (6%)
    all_gather x2, blocking collectives, on_device(): lax.all_gather(amps_now.astype(jnp.bfloat16), 'orb', axis=0, tiled=True)  20.6 us
    reduce_scatter x2, waiting for transfers between devices, on_device(): lax.psum_scatter(jnp.einsum('pqa,pqb->pab', first_projected, second_proje...  17.6 us
    dot_general x2, matrix products, on_device(): jnp.einsum('pkac,pkdc->pad', half_products, couple_intersection, preferre...  8.08 us
    ppermute x2, starting transfers between devices, extended(): lax.ppermute(lax.slice_in_dim(block, 0, width, axis=dim), axis, backward)  6.46 us
    select_n x3, other arithmetic, on_device(): partners = jnp.take(amp_half, partner_ids.reshape(-1), axis=0)  6.39 us
    dot_general x2, matrix products, on_device(): jnp.einsum('pqb,pcb->pqc', fitted_half, pno_maps[:, 0], preferred_element...  5.38 us
    dot_general x2, matrix products, on_device(): jnp.einsum('pqa,pqb->pab', first_projected, second_projected, preferred_e...  5.13 us
    dot_general x2, matrix products, on_device(): jnp.einsum('op,pqc->oqc', onehot, returned, precision=lax.Precision.HIGHEST)  4.54 us
  transfers between devices with their start and end apart: 6, of which 2 were waited for; matrix products, arithmetic and copies ran while one was open for 33% of the time, Pallas kernels for 0%

commit v1 on v0

v1 whole, which is shorter than its diff:
```python
import functools

import jax
import jax.numpy as jnp
from jax import lax
from jax.experimental import pallas as pl
from jax.experimental.pallas import tpu as pltpu
from jax.sharding import PartitionSpec as P

REACH = 1
ITERS = 2
SIDES = 2 * REACH + 1

dress_scale = 0.015

NN = (((1,), (0,)), ((), ()))
NT = (((1,), (1,)), ((), ()))


def dot(left, right, dims=NN):
    return lax.dot_general(left, right, dims, preferred_element_type=jnp.float32)


def kernel(
    ranks,
    groups,
    couple,
    occ_first,
    occ_second,
    occ_energy,
    amplitudes,
    pno_energy,
    inter_hbm,
    maps_hbm,
    orb_hbm,
    out_amps,
    out_dressed,
    inter,
    maps,
    first_t,
    amps_0,
    amps_1,
    window_0,
    window_1,
    second_z,
    parts_out,
    parts_in,
    half,
    fitted,
    amp_send,
    amp_recv,
    win_send,
    win_recv,
    part_send,
    part_recv,
    inter_sem,
    maps_sem,
    orb_sem,
):
    amps = (amps_0, amps_1)
    window = (window_0, window_1)
    own_pairs = amplitudes.shape[0]
    orbs = orb_hbm.shape[0]
    partners = couple.shape[1]
    size = amplitudes.shape[2]
    me = lax.axis_index("orb")
    group = lax.axis_index("pair")
    own = me * own_pairs
    own_rows = pl.ds(own, own_pairs)
    middle = pl.ds(REACH * orbs, orbs)
    bf16 = jnp.bfloat16

    orb_copy = pltpu.make_async_copy(orb_hbm, window[0].at[middle], orb_sem)
    orb_copy.start()
    maps_copies = []
    for part in range(2):
        chunk = pl.ds(part * (maps.shape[0] // 2), maps.shape[0] // 2)
        maps_copies.append(
            pltpu.make_async_copy(maps_hbm.at[chunk], maps.at[chunk], maps_sem.at[part])
        )
        maps_copies[-1].start()
    inter_copies = []
    for i in range(own_pairs):
        inter_copies.append(pltpu.make_async_copy(inter_hbm.at[i], inter.at[i], inter_sem.at[i]))
        inter_copies[-1].start()

    for i in range(own_pairs):
        amps[0][own + i] = amplitudes[i].astype(bf16)

    barrier = pltpu.get_barrier_semaphore()
    for step in range(1, ranks):
        pl.semaphore_signal(
            barrier,
            inc=1,
            device_id={"orb": (me + step) % ranks},
            device_id_type=pl.DeviceIdType.MESH,
        )
    for step in range(1, REACH + 1):
        for shift in (step, groups - step):
            pl.semaphore_signal(
                barrier,
                inc=1,
                device_id={"pair": (group + shift) % groups},
                device_id_type=pl.DeviceIdType.MESH,
            )
    pl.semaphore_wait(barrier, ranks - 1 + 2 * REACH)

    def win_copy(turn, place):
        return pltpu.make_async_remote_copy(
            src_ref=window[turn].at[middle],
            dst_ref=window[turn].at[pl.ds(place * orbs, orbs)],
            send_sem=win_send.at[turn, place],
            recv_sem=win_recv.at[turn, place],
            device_id={"pair": (group + REACH - place + groups) % groups},
            device_id_type=pl.DeviceIdType.MESH,
        )

    def amp_copy(turn, step, i):
        return pltpu.make_async_remote_copy(
            src_ref=amps[turn].at[own + i],
            dst_ref=amps[turn].at[own + i],
            send_sem=amp_send.at[turn, step, i],
            recv_sem=amp_recv.at[turn, step, i],
            device_id={"orb": (me + step) % ranks},
            device_id_type=pl.DeviceIdType.MESH,
        )

    def amp_wait(turn, step):
        for i in range(own_pairs):
            amp_copy(turn, step, i).wait_recv()

    def part_copy(turn, step):
        return pltpu.make_async_remote_copy(
            src_ref=parts_out.at[turn, step],
            dst_ref=parts_in.at[turn, step],
            send_sem=part_send.at[turn, step],
            recv_sem=part_recv.at[turn, step],
            device_id={"orb": (me + step) % ranks},
            device_id_type=pl.DeviceIdType.MESH,
        )

    places = [place for place in range(SIDES) if place != REACH]

    orb_copy.wait()
    for place in places:
        win_copy(0, place).start()
    for step in range(1, ranks):
        for i in range(own_pairs):
            amp_copy(0, step, i).start()

    for copy in maps_copies:
        copy.wait()

    @pl.loop(0, ranks)
    def _(block):
        for i in range(own_pairs):
            first_t[block * own_pairs + i] = maps[block * own_pairs + i, 0].T

    for turn in range(ITERS):
        for place in places:
            win_copy(turn, place).wait_recv()

        @pl.loop(1, ranks + 1)
        def _(ahead):
            step = ahead % ranks
            base = ((me + step) % ranks) * own_pairs
            lefts, rights = [], []
            for i in range(own_pairs):
                pair = base + i
                first = REACH * orbs + occ_first[pair] % orbs
                second = occ_second[pair]
                distance = (second // orbs - group + REACH + groups) % groups
                place = jnp.minimum(distance, SIDES - 1)
                lefts.append(dot(first_t[pair], window[turn][first], NT).astype(bf16))
                rights.append(
                    dot(window[turn][place * orbs + second % orbs], maps[pair, 1]).astype(bf16)
                )
            for i in range(own_pairs):
                second_z[base + i] = rights[i]
                parts_out[turn, step, i] = dot(lefts[i], rights[i]).astype(bf16)

            @pl.when(ahead < ranks)
            def _():
                part_copy(turn, step).start()

        for o in range(orbs):
            fitted[o] = jnp.zeros_like(fitted[o])

        @pl.loop(0, ranks)
        def _(step):
            @pl.when(step > 0)
            def _():
                amp_wait(turn, step)

            base = ((me + ranks - step) % ranks) * own_pairs
            halves = [
                dot(second_z[base + i], amps[turn][base + i]).astype(bf16)
                for i in range(own_pairs)
            ]
            returned = [dot(halves[i], first_t[base + i]) for i in range(own_pairs)]
            for o in range(orbs):
                total = fitted[o]
                for i in range(own_pairs):
                    weight = (occ_first[base + i] % orbs == o).astype(jnp.float32)
                    total += weight * returned[i]
                fitted[o] = total

        for o in range(orbs):
            value = window[0][REACH * orbs + o].astype(jnp.float32) + dress_scale * fitted[o]
            if turn + 1 < ITERS:
                window[turn + 1][REACH * orbs + o] = value.astype(bf16)
            else:
                out_dressed[o] = value
        if turn + 1 < ITERS:
            for place in places:
                win_copy(turn + 1, place).start()

        if turn == 0:
            for copy in inter_copies:
                copy.wait()

        @pl.loop(0, own_pairs)
        def _(i):
            for k in range(partners):
                partner = couple[i, k] % (ranks * own_pairs)
                half[i, :, k * size : (k + 1) * size] = dot(
                    inter[i, k], amps[turn][partner]
                ).astype(bf16)
            coupled = None
            for k in range(0, partners, 2):
                right = jnp.concatenate([inter[i, k], inter[i, k + 1]], axis=1)
                term = dot(half[i, :, k * size : (k + 2) * size], right, NT)
                coupled = term if coupled is None else coupled + term

            @pl.when(i == 0)
            def _():
                for step in range(1, ranks):
                    part_copy(turn, step).wait_recv()

            total = parts_out[turn, 0, i].astype(jnp.float32)
            for step in range(1, ranks):
                total += parts_in[turn, step, i].astype(jnp.float32)
            rows = jnp.broadcast_to(pno_energy[pl.ds(i, 1), :], (size, size))
            denominator = rows + rows.T
            denominator -= occ_energy[occ_first[own + i]]
            denominator -= occ_energy[occ_second[own + i]]
            value = -(total + coupled) / denominator
            if turn + 1 < ITERS:
                amps[turn + 1][own + i] = value.astype(bf16)
                for step in range(1, ranks):
                    amp_copy(turn + 1, step, i).start()
            else:
                out_amps[i] = value

    for turn in range(ITERS):
        for place in places:
            win_copy(turn, place).wait_send()
        for step in range(1, ranks):
            part_copy(turn, step).wait_send()
            for i in range(own_pairs):
                amp_copy(turn, step, i).wait_send()


def on_device(
    ranks,
    groups,
    amplitudes,
    couple,
    occ_first,
    occ_second,
    couple_intersection,
    pno_maps,
    orbital_blocks,
    pno_energy,
    occ_energy,
):
    own_pairs, size, _ = amplitudes.shape
    group_pairs = occ_first.shape[0]
    orbs, rows, virtuals = orbital_blocks.shape
    partners = couple.shape[1]
    bf16 = jnp.bfloat16
    smem = pl.BlockSpec(memory_space=pltpu.SMEM)
    vmem = pl.BlockSpec(memory_space=pltpu.VMEM)
    hbm = pl.BlockSpec(memory_space=pl.ANY)
    dma = pltpu.SemaphoreType.DMA
    return pl.pallas_call(
        functools.partial(kernel, ranks, groups),
        out_shape=(
            jax.ShapeDtypeStruct(amplitudes.shape, jnp.float32),
            jax.ShapeDtypeStruct(orbital_blocks.shape, jnp.float32),
        ),
        in_specs=[smem] * 4 + [vmem] * 2 + [hbm] * 3,
        out_specs=(vmem, vmem),
        scratch_shapes=[
            pltpu.VMEM(couple_intersection.shape, bf16),
            pltpu.VMEM(pno_maps.shape, bf16),
            pltpu.VMEM((group_pairs, size, virtuals), bf16),
            pltpu.VMEM((group_pairs, size, size), bf16),
            pltpu.VMEM((group_pairs, size, size), bf16),
            pltpu.VMEM((SIDES * orbs, rows, virtuals), bf16),
            pltpu.VMEM((SIDES * orbs, rows, virtuals), bf16),
            pltpu.VMEM((group_pairs, rows, size), bf16),
            pltpu.VMEM((ITERS, ranks, own_pairs, size, size), bf16),
            pltpu.VMEM((ITERS, ranks, own_pairs, size, size), bf16),
            pltpu.VMEM((own_pairs, size, partners * size), bf16),
            pltpu.VMEM((orbs, rows, virtuals), jnp.float32),
            dma((ITERS, ranks, own_pairs)),
            dma((ITERS, ranks, own_pairs)),
            dma((ITERS, SIDES)),
            dma((ITERS, SIDES)),
            dma((ITERS, ranks)),
            dma((ITERS, ranks)),
            dma((own_pairs,)),
            dma((2,)),
            dma,
        ],
        compiler_params=pltpu.CompilerParams(
            collective_id=0, has_side_effects=True, vmem_limit_bytes=48 * 2**20
        ),
    )(
        couple,
        occ_first,
        occ_second,
        occ_energy,
        amplitudes,
        pno_energy,
        couple_intersection,
        pno_maps,
        orbital_blocks,
    )


def solution(mesh):
    return jax.shard_map(
        functools.partial(on_device, mesh.shape["orb"], mesh.shape["pair"]),
        mesh=mesh,
        in_specs=(
            P(("pair", "orb"), None, None),
            P(("pair", "orb"), None),
            P("pair"),
            P("pair"),
            P(("pair", "orb"), None, None, None),
            P("pair", None, None, None),
            P("pair", "orb", None),
            P(("pair", "orb"), None),
            P(),
        ),
        out_specs=(P(("pair", "orb"), None, None), P("pair", "orb", None)),
        check_vma=False,
    )
```

time: 108 us -> 45.6 us (0.42)
  Pallas kernels: 0 us -> 35.2 us
  matrix products: 26.3 us -> 0 us
  blocking collectives: 20.6 us -> 0 us
  waiting for transfers between devices: 17.7 us -> 0 us
  between operations: 14.2 us -> 0.66 us
  other arithmetic: 9.95 us -> 0 us
  starting transfers between devices: 6.54 us -> 0 us
  local copies, waits for them, and re-layouts: 12 us -> 9.4 us
    pallas_call x0 -> x1, Pallas kernels: none -> 35.2 us  [on_device(): pl.pallas_call(functools.partial(kernel, ranks, groups), out_shape=(jax.S...]
    dot_general x10 -> x0, matrix products: 26.3 us -> none  [the longest x2 8.08 us: on_device(): jnp.einsum('pkac,pkdc->pad', half_products, couple_intersection, preferre...]
    all_gather x2 -> x0, blocking collectives: 20.6 us -> none  [on_device(): lax.all_gather(amps_now.astype(jnp.bfloat16), 'orb', axis=0, tiled=True)]
    reduce_scatter x2 -> x0, waiting for transfers between devices: 17.6 us -> none  [on_device(): lax.psum_scatter(jnp.einsum('pqa,pqb->pab', first_projected, second_proje...]
    gather x6 -> x0, local copies, waits for them, and re-layouts: 10.9 us -> none  [the longest x2 4.33 us: on_device(): partners = jnp.take(amp_half, partner_ids.reshape(-1), axis=0)]
    unnamed x13 -> x20, local copies, waits for them, and re-layouts: 0.76 us -> 9.4 us
    select_n x5 -> x0, other arithmetic: 7.08 us -> none  [the longest x3 6.39 us: on_device(): partners = jnp.take(amp_half, partner_ids.reshape(-1), axis=0)]
    ppermute x4 -> x0, starting transfers between devices: 6.46 us -> none  [the longest x2 6.46 us: extended(): lax.ppermute(lax.slice_in_dim(block, 0, width, axis=dim), axis, backward)]
  transfers between devices with their start and end apart: 6 -> 0, of which waited for: 2 -> 0; matrix products, arithmetic and copies ran while one was open for 33% -> 0% of each run, Pallas kernels for 0% -> 0%
where the time goes in v1:
time: 45.6 us; the launch traced here: 45.3 us
  Pallas kernels  35.2 us (77%)
  local copies, waits for them, and re-layouts  9.4 us (21%)
  between operations  0.66 us (1%)
    pallas_call x1, Pallas kernels, on_device(): pl.pallas_call(functools.partial(kernel, ranks, groups), out_shape=(jax.S...  35.2 us
    unnamed x20, local copies, waits for them, and re-layouts  9.4 us

profile of v1, /device:TPU:0, one launch (start us, length us, event | category | flops | bytes accessed | tf_op | source)
XLA Modules:
  0.0 45.3 jit_solution(3744637340466289692)
XLA Ops:
  0.6 0.0 copy-start
  0.6 1.6 %copy-done = bf16[4,16,128,128]{3,2,1,0:T(8,128)(2,1)S(1)} copy-done((bf16[4,16,128,128]{3,2,1,0:T(8,128)(2,1)S(1)}, bf16[4,16,128,128]{3,2,1,0:T(8,128)(2,1)}, u32[]{:S(2)}) %copy-start) | copy-done | bytes 2097176
  2.2 0.0 copy-start.1
  2.2 1.2 %copy-done.1 = bf16[16,2,128,128]{3,2,1,0:T(8,128)(2,1)S(1)} copy-done((bf16[16,2,128,128]{3,2,1,0:T(8,128)(2,1)S(1)}, bf16[16,2,128,128]{3,2,1,0:T(8,128)(2,1)}, u32[]{:S(2)}) %copy-start.1) | copy-done | bytes 1048600
  3.5 0.0 copy-start.2
  3.5 0.9 %copy-done.2 = f32[4,128,128]{2,1,0:T(8,128)S(1)} copy-done((f32[4,128,128]{2,1,0:T(8,128)S(1)}, f32[4,128,128]{2,1,0:T(8,128)}, u32[]{:S(2)}) %copy-start.2) | copy-done | bytes 262168
  4.4 0.0 copy-start.3
  4.4 0.9 %copy-done.3 = bf16[4,128,128]{2,1,0:T(8,128)(2,1)S(1)} copy-done((bf16[4,128,128]{2,1,0:T(8,128)(2,1)S(1)}, bf16[4,128,128]{2,1,0:T(8,128)(2,1)}, u32[]{:S(2)}) %copy-start.3) | copy-done | bytes 131096
  5.3 0.0 copy-start.4
  5.3 0.7 %copy-done.4 = s32[4,16]{1,0:T(4,128)S(1)} copy-done((s32[4,16]{1,0:T(4,128)S(1)}, s32[4,16]{1,0:T(4,128)}, u32[]{:S(2)}) %copy-start.4) | copy-done | bytes 280
  6.0 0.0 copy-start.5
  6.0 0.7 %copy-done.5 = f32[4,128]{1,0:T(4,128)S(1)} copy-done((f32[4,128]{1,0:T(4,128)S(1)}, f32[4,128]{1,0:T(4,128)}, u32[]{:S(2)}) %copy-start.5) | copy-done | bytes 2072
  6.7 0.0 copy-start.6
  6.7 0.7 %copy-done.6 = s32[16]{0:T(128)S(1)} copy-done((s32[16]{0:T(128)S(1)}, s32[16]{0:T(128)}, u32[]{:S(2)}) %copy-start.6) | copy-done | bytes 88
  7.3 0.0 copy-start.7
  7.3 0.7 %copy-done.7 = s32[16]{0:T(128)S(1)} copy-done((s32[16]{0:T(128)S(1)}, s32[16]{0:T(128)}, u32[]{:S(2)}) %copy-start.7) | copy-done | bytes 88
  8.0 0.0 copy-start.8
  8.0 0.7 %copy-done.8 = f32[32]{0:T(128)S(1)} copy-done((f32[32]{0:T(128)S(1)}, f32[32]{0:T(128)}, u32[]{:S(2)}) %copy-start.8) | copy-done | bytes 152
  8.6 35.2 %shard_map.104 = (f32[4,128,128]{2,1,0:T(8,128)S(1)}, f32[4,128,128]{2,1,0:T(8,128)S(1)}) custom-call(s32[4,16]{1,0:T(4,128)S(1)} %copy-done.4, s32[16]{0:T(128)S(1)} %copy-done.6, s32[16]{0:T(128)S(1)} %copy-done.7, f32[32]{0:T(128)S(1)} %copy-done.8, f32[4,128,128]{2,1,0:T(8,128)S(1)} %copy-done.2, f32[4,128]{1,0:T(4,128)S(1)} %copy-done.5, ...), custom_call_target="tpu_custom_call" | custom-call | tf_op jit(solution)/shard_map/pallas_call | solution.py:286
  43.8 0.7 %copy.13 = f32[4,128,128]{2,1,0:T(8,128)} copy(f32[4,128,128]{2,1,0:T(8,128)S(1)} %get-tuple-element.4) | data formatting | bytes 524288
  44.5 0.7 %copy.14 = f32[4,128,128]{2,1,0:T(8,128)} copy(f32[4,128,128]{2,1,0:T(8,128)S(1)} %get-tuple-element.5) | data formatting | bytes 524288
Async XLA Ops:
  0.6 1.6 %copy-start = (bf16[4,16,128,128]{3,2,1,0:T(8,128)(2,1)S(1)}, bf16[4,16,128,128]{3,2,1,0:T(8,128)(2,1)}, u32[]{:S(2)}) copy-start(bf16[4,16,128,128]{3,2,1,0:T(8,128)(2,1)} %inter_hbm.1) | copy-start | bytes 6291460
  2.2 1.2 %copy-start.1 = (bf16[16,2,128,128]{3,2,1,0:T(8,128)(2,1)S(1)}, bf16[16,2,128,128]{3,2,1,0:T(8,128)(2,1)}, u32[]{:S(2)}) copy-start(bf16[16,2,128,128]{3,2,1,0:T(8,128)(2,1)} %maps_hbm.1) | copy-start | bytes 3145732
  3.5 0.9 %copy-start.2 = (f32[4,128,128]{2,1,0:T(8,128)S(1)}, f32[4,128,128]{2,1,0:T(8,128)}, u32[]{:S(2)}) copy-start(f32[4,128,128]{2,1,0:T(8,128)} %amplitudes.1) | copy-start | bytes 786436
  4.4 0.9 %copy-start.3 = (bf16[4,128,128]{2,1,0:T(8,128)(2,1)S(1)}, bf16[4,128,128]{2,1,0:T(8,128)(2,1)}, u32[]{:S(2)}) copy-start(bf16[4,128,128]{2,1,0:T(8,128)(2,1)} %orb_hbm.1) | copy-start | bytes 393220
  5.3 0.7 %copy-start.4 = (s32[4,16]{1,0:T(4,128)S(1)}, s32[4,16]{1,0:T(4,128)}, u32[]{:S(2)}) copy-start(s32[4,16]{1,0:T(4,128)} %couple.1) | copy-start | bytes 772
  6.0 0.7 %copy-start.5 = (f32[4,128]{1,0:T(4,128)S(1)}, f32[4,128]{1,0:T(4,128)}, u32[]{:S(2)}) copy-start(f32[4,128]{1,0:T(4,128)} %pno_energy.1) | copy-start | bytes 6148
  6.7 0.7 %copy-start.6 = (s32[16]{0:T(128)S(1)}, s32[16]{0:T(128)}, u32[]{:S(2)}) copy-start(s32[16]{0:T(128)} %occ_first.1) | copy-start | bytes 196
  7.3 0.7 %copy-start.7 = (s32[16]{0:T(128)S(1)}, s32[16]{0:T(128)}, u32[]{:S(2)}) copy-start(s32[16]{0:T(128)} %occ_second.1) | copy-start | bytes 196
  8.0 0.7 %copy-start.8 = (f32[32]{0:T(128)S(1)}, f32[32]{0:T(128)}, u32[]{:S(2)}) copy-start(f32[32]{0:T(128)} %occ_energy.1) | copy-start | bytes 388

commit v2 on v1

--- a/solution.py
+++ b/solution.py
@@ -281,7 +281,7 @@
     bf16 = jnp.bfloat16
     smem = pl.BlockSpec(memory_space=pltpu.SMEM)
     vmem = pl.BlockSpec(memory_space=pltpu.VMEM)
-    hbm = pl.BlockSpec(memory_space=pl.ANY)
+    hbm = pl.BlockSpec(memory_space=pltpu.HBM)
     dma = pltpu.SemaphoreType.DMA
     return pl.pallas_call(
         functools.partial(kernel, ranks, groups),
@@ -315,7 +315,7 @@
             dma,
         ],
         compiler_params=pltpu.CompilerParams(
-            collective_id=0, has_side_effects=True, vmem_limit_bytes=48 * 2**20
+            collective_id=0, has_side_effects=True, vmem_limit_bytes=67043328
         ),
     )(
         couple,

time: 45.6 us -> 39.9 us (0.87)
  local copies, waits for them, and re-layouts: 9.4 us -> 3.34 us
  Pallas kernels: 35.2 us -> 35.8 us
    unnamed x20 -> x2, local copies, waits for them, and re-layouts: 9.4 us -> 3.34 us
    pallas_call x1, Pallas kernels: 35.2 us -> 35.8 us  [on_device(): pl.pallas_call(functools.partial(kernel, ranks, groups), out_shape=(jax.S...]
where the time goes in v2:
time: 39.9 us; the launch traced here: 39.7 us
  Pallas kernels  35.8 us (90%)
  local copies, waits for them, and re-layouts  3.34 us (8%)
  between operations  0.64 us (2%)
    pallas_call x1, Pallas kernels, on_device(): pl.pallas_call(functools.partial(kernel, ranks, groups), out_shape=(jax.S...  35.8 us
    unnamed x2, local copies, waits for them, and re-layouts  3.34 us

profile of v2, /device:TPU:0, one launch (start us, length us, event | category | flops | bytes accessed | tf_op | source)
XLA Modules:
  0.0 39.7 jit_solution(755002842438899156)
XLA Ops:
  0.6 35.8 %shard_map.104 = (f32[4,128,128]{2,1,0:T(8,128)}, f32[4,128,128]{2,1,0:T(8,128)}) custom-call(s32[4,16]{1,0:T(4,128)} %couple.1, s32[16]{0:T(128)} %occ_first.1, s32[16]{0:T(128)} %occ_second.1, f32[32]{0:T(128)} %occ_energy.1, f32[4,128,128]{2,1,0:T(8,128)} %amplitudes.1, f32[4,128]{1,0:T(4,128)} %pno_energy.1, bf16[4,16,128,128]{3,2,1,0:T(8,128)(2,1)} %inter_hbm.1, ...), custom_call_target="tpu_custom_call" | custom-call | tf_op jit(solution)/shard_map/pallas_call | solution.py:286
  36.4 1.7 %copy.13 = f32[4,128,128]{2,1,0:T(8,128)} copy(f32[4,128,128]{2,1,0:T(8,128)} %get-tuple-element.4) | data formatting | bytes 524288
  38.1 1.7 %copy.14 = f32[4,128,128]{2,1,0:T(8,128)} copy(f32[4,128,128]{2,1,0:T(8,128)} %get-tuple-element.5) | data formatting | bytes 524288

commit v3 on v2

--- a/solution.py
+++ b/solution.py
@@ -69,6 +69,17 @@
     own_rows = pl.ds(own, own_pairs)
     middle = pl.ds(REACH * orbs, orbs)
     bf16 = jnp.bfloat16
+    square = ranks == 4 and own_pairs % 2 == 0
+    low = own_pairs // 2
+    lower, upper = pl.ds(0, low), pl.ds(low, own_pairs - low)
+
+    def target(step):
+        if square:
+            return (me // 2 + step // 2) % 2 * 2 + (me + step) % 2
+        return (me + step) % ranks
+
+    def source(step):
+        return target(step) if square else (me + ranks - step) % ranks
 
     orb_copy = pltpu.make_async_copy(orb_hbm, window[0].at[middle], orb_sem)
     orb_copy.start()
@@ -121,32 +132,88 @@
             dst_ref=amps[turn].at[own + i],
             send_sem=amp_send.at[turn, step, i],
             recv_sem=amp_recv.at[turn, step, i],
-            device_id={"orb": (me + step) % ranks},
+            device_id={"orb": target(step)},
             device_id_type=pl.DeviceIdType.MESH,
         )
+
+    def amp_relay(turn, i):
+        via, onto = (1, 2) if i < low else (2, 1)
+        place = target(via) * own_pairs + i
+        return pltpu.make_async_remote_copy(
+            src_ref=amps[turn].at[place],
+            dst_ref=amps[turn].at[place],
+            send_sem=amp_send.at[turn, 3, i],
+            recv_sem=amp_recv.at[turn, 3, i],
+            device_id={"orb": target(onto)},
+            device_id_type=pl.DeviceIdType.MESH,
+        )
+
+    def relay_all(turn):
+        for i in range(low):
+            for j, via in ((i, 1), (low + i, 2)):
+                amp_copy(turn, via, j).wait_recv()
+                amp_relay(turn, j).start()
 
     def amp_wait(turn, step):
         for i in range(own_pairs):
-            amp_copy(turn, step, i).wait_recv()
-
-    def part_copy(turn, step):
+            if not square:
+                amp_copy(turn, step, i).wait_recv()
+            elif step == 3:
+                amp_relay(turn, i).wait_recv()
+            elif (i < low) != (step == 1):
+                amp_copy(turn, step, i).wait_recv()
+
+    def part_send_to(turn, step, onto, half_of, sem):
+        rows = (slice(None), lower, upper)[half_of] if half_of else pl.ds(0, own_pairs)
         return pltpu.make_async_remote_copy(
-            src_ref=parts_out.at[turn, step],
-            dst_ref=parts_in.at[turn, step],
-            send_sem=part_send.at[turn, step],
-            recv_sem=part_recv.at[turn, step],
-            device_id={"orb": (me + step) % ranks},
+            src_ref=parts_out.at[turn, step, rows],
+            dst_ref=parts_in.at[turn, step, rows],
+            send_sem=part_send.at[turn, sem],
+            recv_sem=part_recv.at[turn, sem],
+            device_id={"orb": target(onto)},
             device_id_type=pl.DeviceIdType.MESH,
         )
+
+    if square:
+        part_first = {1: [(1, 1, 1, 0)], 2: [(2, 2, 2, 1)], 3: [(3, 1, 1, 2), (3, 2, 2, 3)]}
+        part_second = [(2, 2, 1, 4), (1, 1, 2, 5)]
+        part_last = [(1, 1, 1, 0), (2, 2, 2, 1)] + part_second
+        part_all = part_last + part_first[3]
+        terms = (1, 2)
+    else:
+        part_first = {step: [(step, step, 0, step)] for step in range(1, ranks)}
+        part_second = []
+        part_last = part_all = [entry for step in part_first for entry in part_first[step]]
+        terms = range(1, ranks)
+
+    def part_forward(turn):
+        for arrived, entry in zip((part_first[3] if square else []), part_second):
+            part_send_to(turn, *arrived).wait_recv()
+            step, _, half_of, _ = entry
+            for i in range(low):
+                i = i if half_of == 1 else low + i
+                total = parts_out[turn, step, i].astype(jnp.float32)
+                total += parts_in[turn, 3, i].astype(jnp.float32)
+                parts_out[turn, step, i] = total.astype(bf16)
+            part_send_to(turn, *entry).start()
+
+    def amp_start(turn, i):
+        for step in (1, 2) if square else range(1, ranks):
+            amp_copy(turn, step, i).start()
 
     places = [place for place in range(SIDES) if place != REACH]
 
     orb_copy.wait()
     for place in places:
         win_copy(0, place).start()
-    for step in range(1, ranks):
+    if square:
         for i in range(own_pairs):
-            amp_copy(0, step, i).start()
+            for step in (1, 2):
+                j = i if step == 1 else (i + low) % own_pairs
+                amp_copy(0, step, j).start()
+    else:
+        for i in range(own_pairs):
+            amp_start(0, i)
 
     for copy in maps_copies:
         copy.wait()
@@ -159,11 +226,13 @@
     for turn in range(ITERS):
         for place in places:
             win_copy(turn, place).wait_recv()
+        if square and turn == 0:
+            relay_all(turn)
 
         @pl.loop(1, ranks + 1)
         def _(ahead):
-            step = ahead % ranks
-            base = ((me + step) % ranks) * own_pairs
+            step = ranks - ahead
+            base = target(step) * own_pairs
             lefts, rights = [], []
             for i in range(own_pairs):
                 pair = base + i
@@ -179,20 +248,40 @@
                 second_z[base + i] = rights[i]
                 parts_out[turn, step, i] = dot(lefts[i], rights[i]).astype(bf16)
 
-            @pl.when(ahead < ranks)
-            def _():
-                part_copy(turn, step).start()
+            if square:
+                for at in part_first:
+
+                    @pl.when(step == at)
+                    def _(at=at):
+                        for entry in part_first[at]:
+                            part_send_to(turn, *entry).start()
+            else:
+
+                @pl.when(step > 0)
+                def _():
+                    part_send_to(turn, step, step, 0, step).start()
+
+        if square and turn > 0:
+            relay_all(turn)
 
         for o in range(orbs):
             fitted[o] = jnp.zeros_like(fitted[o])
 
         @pl.loop(0, ranks)
         def _(step):
-            @pl.when(step > 0)
-            def _():
-                amp_wait(turn, step)
-
-            base = ((me + ranks - step) % ranks) * own_pairs
+            if square:
+                for at in range(1, ranks):
+
+                    @pl.when(step == at)
+                    def _(at=at):
+                        amp_wait(turn, at)
+            else:
+
+                @pl.when(step > 0)
+                def _():
+                    amp_wait(turn, step)
+
+            base = source(step) * own_pairs
             halves = [
                 dot(second_z[base + i], amps[turn][base + i]).astype(bf16)
                 for i in range(own_pairs)
@@ -214,6 +303,8 @@
         if turn + 1 < ITERS:
             for place in places:
                 win_copy(turn + 1, place).start()
+
+        part_forward(turn)
 
         if turn == 0:
             for copy in inter_copies:
@@ -234,11 +325,11 @@
 
             @pl.when(i == 0)
             def _():
-                for step in range(1, ranks):
-                    part_copy(turn, step).wait_recv()
+                for entry in part_last:
+                    part_send_to(turn, *entry).wait_recv()
 
             total = parts_out[turn, 0, i].astype(jnp.float32)
-            for step in range(1, ranks):
+            for step in terms:
                 total += parts_in[turn, step, i].astype(jnp.float32)
             rows = jnp.broadcast_to(pno_energy[pl.ds(i, 1), :], (size, size))
             denominator = rows + rows.T
@@ -247,18 +338,21 @@
             value = -(total + coupled) / denominator
             if turn + 1 < ITERS:
                 amps[turn + 1][own + i] = value.astype(bf16)
-                for step in range(1, ranks):
-                    amp_copy(turn + 1, step, i).start()
+                amp_start(turn + 1, i)
             else:
                 out_amps[i] = value
 
     for turn in range(ITERS):
         for place in places:
             win_copy(turn, place).wait_send()
-        for step in range(1, ranks):
-            part_copy(turn, step).wait_send()
-            for i in range(own_pairs):
-                amp_copy(turn, step, i).wait_send()
+        for entry in part_all:
+            part_send_to(turn, *entry).wait_send()
+        for i in range(own_pairs):
+            for step in range(1, ranks):
+                if square and step == 3:
+                    amp_relay(turn, i).wait_send()
+                else:
+                    amp_copy(turn, step, i).wait_send()
 
 
 def on_device(
@@ -308,8 +402,8 @@
             dma((ITERS, ranks, own_pairs)),
             dma((ITERS, SIDES)),
             dma((ITERS, SIDES)),
-            dma((ITERS, ranks)),
-            dma((ITERS, ranks)),
+            dma((ITERS, ranks + 2)),
+            dma((ITERS, ranks + 2)),
             dma((own_pairs,)),
             dma((2,)),
             dma,

time: 39.9 us -> 39 us (0.977)
  Pallas kernels: 35.8 us -> 34.8 us
    pallas_call x1, Pallas kernels: 35.8 us -> 34.8 us  [on_device(): pl.pallas_call(functools.partial(kernel, ranks, groups), out_shape=(jax.S...]
where the time goes in v3:
time: 39 us; the launch traced here: 38.8 us
  Pallas kernels  34.8 us (89%)
  local copies, waits for them, and re-layouts  3.34 us (9%)
  between operations  0.64 us (2%)
    pallas_call x1, Pallas kernels, on_device(): pl.pallas_call(functools.partial(kernel, ranks, groups), out_shape=(jax.S...  34.8 us
    unnamed x2, local copies, waits for them, and re-layouts  3.34 us

profile of v3, /device:TPU:0, one launch (start us, length us, event | category | flops | bytes accessed | tf_op | source)
XLA Modules:
  0.0 38.8 jit_solution(5481448378208967254)
XLA Ops:
  0.6 34.8 %shard_map.104 = (f32[4,128,128]{2,1,0:T(8,128)}, f32[4,128,128]{2,1,0:T(8,128)}) custom-call(s32[4,16]{1,0:T(4,128)} %couple.1, s32[16]{0:T(128)} %occ_first.1, s32[16]{0:T(128)} %occ_second.1, f32[32]{0:T(128)} %occ_energy.1, f32[4,128,128]{2,1,0:T(8,128)} %amplitudes.1, f32[4,128]{1,0:T(4,128)} %pno_energy.1, bf16[4,16,128,128]{3,2,1,0:T(8,128)(2,1)} %inter_hbm.1, ...), custom_call_target="tpu_custom_call" | custom-call | tf_op jit(solution)/shard_map/pallas_call | solution.py:380
  35.4 1.7 %copy.13 = f32[4,128,128]{2,1,0:T(8,128)} copy(f32[4,128,128]{2,1,0:T(8,128)} %get-tuple-element.4) | data formatting | bytes 524288
  37.1 1.7 %copy.14 = f32[4,128,128]{2,1,0:T(8,128)} copy(f32[4,128,128]{2,1,0:T(8,128)} %get-tuple-element.5) | data formatting | bytes 524288

commit v4 on v3

--- a/solution.py
+++ b/solution.py
@@ -24,17 +24,23 @@
 def kernel(
     ranks,
     groups,
+    couple_hbm,
+    first_hbm,
+    second_hbm,
+    energy_hbm,
+    amps_hbm,
+    pno_hbm,
+    inter_hbm,
+    maps_hbm,
+    orb_hbm,
+    out_amps,
+    out_dressed,
     couple,
     occ_first,
     occ_second,
     occ_energy,
     amplitudes,
     pno_energy,
-    inter_hbm,
-    maps_hbm,
-    orb_hbm,
-    out_amps,
-    out_dressed,
     inter,
     maps,
     first_t,
@@ -56,10 +62,11 @@
     inter_sem,
     maps_sem,
     orb_sem,
+    small_sem,
 ):
     amps = (amps_0, amps_1)
     window = (window_0, window_1)
-    own_pairs = amplitudes.shape[0]
+    own_pairs = amps_hbm.shape[0]
     orbs = orb_hbm.shape[0]
     partners = couple.shape[1]
     size = amplitudes.shape[2]
@@ -83,6 +90,21 @@
 
     orb_copy = pltpu.make_async_copy(orb_hbm, window[0].at[middle], orb_sem)
     orb_copy.start()
+    small_copies = [
+        pltpu.make_async_copy(source_ref, target_ref, small_sem.at[at])
+        for at, (source_ref, target_ref) in enumerate(
+            (
+                (amps_hbm, amplitudes),
+                (couple_hbm, couple),
+                (first_hbm, occ_first),
+                (second_hbm, occ_second),
+                (energy_hbm, occ_energy),
+                (pno_hbm, pno_energy),
+            )
+        )
+    ]
+    for copy in small_copies:
+        copy.start()
     maps_copies = []
     for part in range(2):
         chunk = pl.ds(part * (maps.shape[0] // 2), maps.shape[0] // 2)
@@ -94,9 +116,6 @@
     for i in range(own_pairs):
         inter_copies.append(pltpu.make_async_copy(inter_hbm.at[i], inter.at[i], inter_sem.at[i]))
         inter_copies[-1].start()
-
-    for i in range(own_pairs):
-        amps[0][own + i] = amplitudes[i].astype(bf16)
 
     barrier = pltpu.get_barrier_semaphore()
     for step in range(1, ranks):
@@ -114,6 +133,9 @@
                 device_id={"pair": (group + shift) % groups},
                 device_id_type=pl.DeviceIdType.MESH,
             )
+    small_copies[0].wait()
+    for i in range(own_pairs):
+        amps[0][own + i] = amplitudes[i].astype(bf16)
     pl.semaphore_wait(barrier, ranks - 1 + 2 * REACH)
 
     def win_copy(turn, place):
@@ -215,7 +237,7 @@
         for i in range(own_pairs):
             amp_start(0, i)
 
-    for copy in maps_copies:
+    for copy in maps_copies + small_copies[1:]:
         copy.wait()
 
     @pl.loop(0, ranks)
@@ -373,19 +395,24 @@
     orbs, rows, virtuals = orbital_blocks.shape
     partners = couple.shape[1]
     bf16 = jnp.bfloat16
-    smem = pl.BlockSpec(memory_space=pltpu.SMEM)
     vmem = pl.BlockSpec(memory_space=pltpu.VMEM)
     hbm = pl.BlockSpec(memory_space=pltpu.HBM)
     dma = pltpu.SemaphoreType.DMA
     return pl.pallas_call(
         functools.partial(kernel, ranks, groups),
         out_shape=(
-            jax.ShapeDtypeStruct(amplitudes.shape, jnp.float32),
-            jax.ShapeDtypeStruct(orbital_blocks.shape, jnp.float32),
+            pltpu.VMEM(amplitudes.shape, jnp.float32),
+            pltpu.VMEM(orbital_blocks.shape, jnp.float32),
         ),
-        in_specs=[smem] * 4 + [vmem] * 2 + [hbm] * 3,
+        in_specs=[hbm] * 9,
         out_specs=(vmem, vmem),
         scratch_shapes=[
+            pltpu.SMEM(couple.shape, couple.dtype),
+            pltpu.SMEM(occ_first.shape, occ_first.dtype),
+            pltpu.SMEM(occ_second.shape, occ_second.dtype),
+            pltpu.SMEM(occ_energy.shape, occ_energy.dtype),
+            pltpu.VMEM(amplitudes.shape, amplitudes.dtype),
+            pltpu.VMEM(pno_energy.shape, pno_energy.dtype),
             pltpu.VMEM(couple_intersection.shape, bf16),
             pltpu.VMEM(pno_maps.shape, bf16),
             pltpu.VMEM((group_pairs, size, virtuals), bf16),
@@ -407,11 +434,13 @@
             dma((own_pairs,)),
             dma((2,)),
             dma,
+            dma((6,)),
         ],
         compiler_params=pltpu.CompilerParams(
-            collective_id=0, has_side_effects=True, vmem_limit_bytes=67043328
+            collective_id=0, has_side_effects=True, vmem_limit_bytes=67043328 - 4096 * 1024
         ),
     )(
+        *(pltpu.with_memory_space_constraint(x, pltpu.HBM) for x in (
         couple,
         occ_first,
         occ_second,
@@ -421,6 +450,7 @@
         couple_intersection,
         pno_maps,
         orbital_blocks,
+        ))
     )
 
 

time: 39 us -> 35.3 us (0.905)
  local copies, waits for them, and re-layouts: 3.34 us -> 1.41 us
  Pallas kernels: 34.8 us -> 33.1 us
    unnamed x2, local copies, waits for them, and re-layouts: 3.34 us -> 1.41 us
    pallas_call x1, Pallas kernels: 34.8 us -> 33.1 us  [on_device(): pl.pallas_call(functools.partial(kernel, ranks, groups), out_shape=(pltpu...]
where the time goes in v4:
time: 35.3 us; the launch traced here: 35.2 us
  Pallas kernels  33.1 us (94%)
  local copies, waits for them, and re-layouts  1.41 us (4%)
  between operations  0.64 us (2%)
    pallas_call x1, Pallas kernels, on_device(): pl.pallas_call(functools.partial(kernel, ranks, groups), out_shape=(pltpu...  33.1 us
    unnamed x2, local copies, waits for them, and re-layouts  1.41 us

profile of v4, /device:TPU:0, one launch (start us, length us, event | category | flops | bytes accessed | tf_op | source)
XLA Modules:
  0.0 35.2 jit_solution(15757355305187622441)
XLA Ops:
  0.6 33.1 %shard_map.104 = (f32[4,128,128]{2,1,0:T(8,128)S(1)}, f32[4,128,128]{2,1,0:T(8,128)S(1)}) custom-call(s32[4,16]{1,0:T(4,128)} %couple_hbm.1, s32[16]{0:T(128)} %first_hbm.1, s32[16]{0:T(128)} %second_hbm.1, f32[32]{0:T(128)} %energy_hbm.1, f32[4,128,128]{2,1,0:T(8,128)} %amps_hbm.1, f32[4,128]{1,0:T(4,128)} %pno_hbm.1, bf16[4,16,128,128]{3,2,1,0:T(8,128)(2,1)} %inter_hbm.1, ...), custom_call_target="tpu_custom_call" | custom-call | tf_op jit(solution)/shard_map/pallas_call | solution.py:401
  33.7 0.7 %copy.13 = f32[4,128,128]{2,1,0:T(8,128)} copy(f32[4,128,128]{2,1,0:T(8,128)S(1)} %get-tuple-element.2) | data formatting | bytes 524288
  34.5 0.7 %copy.14 = f32[4,128,128]{2,1,0:T(8,128)} copy(f32[4,128,128]{2,1,0:T(8,128)S(1)} %get-tuple-element.3) | data formatting | bytes 524288
